TPU v7x, 256 devices: a whole 4x4x8 slice. The times are simulated.
256 devices in a mesh: out: 32 (over z, y), inp: 8 (over x, core).
Axes of the slice: x: 4, y: 4, z: 8, core: 2. Of those that a mesh axis runs over, the one named last changes fastest.
Arguments:
- weight: float32 [32, 512, 13824], P(None, 'out', 'inp'), may hold values from -6 to 6
- gradient: bfloat16 [32, 512, 13824], P(None, 'out', 'inp'), may hold values from -60 to 60
- momentum: bfloat16 [32, 512, 13824], P(None, 'out', 'inp'), may hold values from -6 to 6
Outputs:
- weight_next: float32 [32, 512, 13824], P(None, 'out', 'inp')
- momentum_next: bfloat16 [32, 512, 13824], P(None, 'out', 'inp')
All inputs are finite; a program needn't handle non-finite values.
Results may differ from a plain program's by a relative error of at most 0.0039.
Values may be sent and summed in bfloat16 or wider, within the bound.
A program may use at most 64 MiB of HBM per device.

v0:
```python
import functools
import math

import jax
import jax.numpy as jnp
from jax import lax
from jax.experimental import pallas as pl
from jax.experimental.pallas import tpu as pltpu
from jax.sharding import PartitionSpec as P

ITERS = 5
COLS = 13824
BETA = 0.95
EPSILON = 1e-06
COEF_A = 3.4445
COEF_B = -4.775
COEF_C = 2.0315

MESH = pl.DeviceIdType.MESH
BF16 = jnp.bfloat16
F32 = jnp.float32

ZS, YS, INP = 8, 4, 8
OUT = ZS * YS
BATCHES = 2
ROWS = 512
BLOCK = 16
WIDTH = 1792
HALF = WIDTH // BATCHES
GROUP = INP // 2 * BATCHES
PIECES = [(i, j) for i in range(4) for j in range(i, 4)]
TALL = 128 * len(PIECES)
SLICE = TALL // GROUP
VMEM_LIMIT = 50 * 2**20


def dot(a, b):
    return lax.dot_general(a, b, (((1,), (0,)), ((), ())), preferred_element_type=F32)


def dot_t(a, b):
    return lax.dot_general(a, b, (((1,), (1,)), ((), ())), preferred_element_type=F32)


def split(x):
    high = x.astype(BF16)
    return high, (x - high.astype(F32)).astype(BF16)


def product(a, b):
    return dot(a[0][...], b[0][...]) + dot(a[0][...], b[1][...]) + dot(a[1][...], b[0][...])


def put(pair, x):
    high, low = split(x)
    pair[0][...] = high
    pair[1][...] = low


def kernel(
    grad, mom, ret, mom_next, src, held, upd, packed, slots, own, full, factor,
    rh, rl, qh, ql, mh, ml, yh, yl, grad_in, mom_in, mom_out,
    f_send, f_recv, b_send, b_recv, r_send, r_recv, g_send, g_recv, local, load, store,
):
    me = lax.axis_index("out")
    inp = lax.axis_index("inp")
    z, y = me // YS, lax.rem(me, YS)
    team, seat = me // BATCHES, lax.rem(me, BATCHES)
    x, core = inp // 2, lax.rem(inp, 2)
    rank = seat * (INP // 2) + x
    mine = team * BATCHES + core
    width = grad.shape[2]

    loads = [
        pltpu.make_async_copy(grad, grad_in, load.at[0]),
        pltpu.make_async_copy(mom, mom_in, load.at[1]),
    ]
    for copy in loads:
        copy.start()

    def partner(i):
        at = lax.rem(i, OUT) + i // OUT
        t = at // YS
        step = jnp.where(lax.rem(t, 2) == 1, (t + 1) // 2, ZS - t // 2)
        return lax.rem(z + step, ZS) * YS + lax.rem(y + lax.rem(at, YS), YS)

    def mate(j):
        other = lax.rem(rank + j, GROUP)
        return (team * BATCHES + other // (INP // 2), 2 * lax.rem(other, INP // 2) + core), other

    barrier = pltpu.get_barrier_semaphore()

    def greet(i, c):
        dest = lax.rem(me + i, OUT)
        for other in range(2):
            pl.semaphore_signal(barrier, inc=1, device_id=(dest, 2 * x + other), device_id_type=MESH)
        return c

    def greet_mate(j, c):
        pl.semaphore_signal(barrier, inc=1, device_id=mate(j)[0], device_id_type=MESH)
        return c

    lax.fori_loop(1, OUT, greet, 0)
    lax.fori_loop(1, GROUP, greet_mate, 0)
    pl.semaphore_signal(barrier, inc=1, device_id=(me, 2 * x + 1 - core), device_id_type=MESH)

    for copy in loads:
        copy.wait()

    def elementwise(k, c):
        g = grad_in[k].astype(F32)
        moment = BETA * mom_in[k].astype(F32) + g
        mom_out[k] = moment.astype(BF16)
        src[k, :, 0:width] = (g + BETA * moment).astype(BF16)
        src[k, :, width:WIDTH] = jnp.zeros((BLOCK, WIDTH - width), BF16)
        return c

    lax.fori_loop(0, OUT, elementwise, 0)
    keep_moment = pltpu.make_async_copy(mom_out, mom_next, store)
    keep_moment.start()
    pl.semaphore_wait(barrier, 2 * (OUT - 1) + GROUP - 1 + 1)

    def block(dest):
        return pl.ds(pl.multiple_of(dest * BLOCK, BLOCK), BLOCK)

    def half(which):
        return pl.ds(pl.multiple_of(which * HALF, 128), HALF)

    def place(dest):
        return lax.rem(dest // YS - z + ZS, ZS) * YS + lax.rem(lax.rem(dest, YS) - y + YS, YS)

    def forward(b, dest):
        return pltpu.make_async_remote_copy(
            src_ref=src.at[dest // BATCHES * BATCHES + b, :, half(lax.rem(dest, BATCHES))],
            dst_ref=held.at[block(me), half(core)],
            send_sem=f_send.at[b, place(dest)],
            recv_sem=f_recv.at[core, place(dest)],
            device_id=(dest, 2 * x + b),
            device_id_type=MESH,
        )

    def forward_in(other, i):
        return pltpu.make_async_remote_copy(
            src_ref=src.at[0, :, half(0)],
            dst_ref=held.at[block(0), half(0)],
            send_sem=f_send.at[other, i],
            recv_sem=f_recv.at[other, i],
            device_id=(me, 2 * x + 1 - core),
            device_id_type=MESH,
        )

    def backward(b, dest):
        return pltpu.make_async_remote_copy(
            src_ref=upd.at[block(dest), half(b)],
            dst_ref=ret.at[mine, :, half(seat)],
            send_sem=b_send.at[b, place(dest)],
            recv_sem=b_recv.at[core, place(dest)],
            device_id=(dest, 2 * x + b),
            device_id_type=MESH,
        )

    def backward_in(other, i):
        return pltpu.make_async_remote_copy(
            src_ref=upd.at[block(0), half(0)],
            dst_ref=ret.at[0, :, half(0)],
            send_sem=b_send.at[other, i],
            recv_sem=b_recv.at[other, i],
            device_id=(me, 2 * x + 1 - core),
            device_id_type=MESH,
        )

    keep_forward = pltpu.make_async_copy(
        src.at[mine, :, half(seat)], held.at[block(me), half(core)], local.at[0]
    )
    keep_backward = pltpu.make_async_copy(
        upd.at[block(me), half(core)], ret.at[mine, :, half(seat)], local.at[1]
    )

    def each(low, high, do):
        def body(i, c):
            do(i)
            return c

        lax.fori_loop(low, high, body, 0)

    my_slice = pl.ds(pl.multiple_of(rank * SLICE, 16), SLICE)

    def scatter(j):
        device, other = mate(j)
        return pltpu.make_async_remote_copy(
            src_ref=packed.at[pl.ds(pl.multiple_of(other * SLICE, 16), SLICE)],
            dst_ref=slots.at[j],
            send_sem=r_send.at[j],
            recv_sem=r_recv.at[j],
            device_id=device,
            device_id_type=MESH,
        )

    def gather(j):
        device, _ = mate(j)
        return pltpu.make_async_remote_copy(
            src_ref=own,
            dst_ref=full.at[my_slice],
            send_sem=g_send.at[j],
            recv_sem=g_recv.at[j],
            device_id=device,
            device_id_type=MESH,
        )

    for b in range(2):
        each(YS, YS + OUT - 1, lambda i: forward(b, partner(i)).start())
        pl.when(core != b)(lambda: forward(b, me).start())
    keep_forward.start()

    def others(do):
        for other in range(2):
            each(1, OUT, lambda i: do(other, i))
            pl.when(core != other)(lambda: do(other, 0))

    keep_forward.wait()
    others(lambda other, i: forward_in(other, i).wait_recv())
    top = dot_t(held[0:256, :], held[...]).astype(BF16)
    low = dot_t(held[256:512, :], held[256:512, :]).astype(BF16)
    for n, (i, j) in enumerate(PIECES):
        rows, cols = (128 * i, 128 * j) if i < 2 else (128 * i - 256, 128 * j - 256)
        packed[128 * n : 128 * n + 128, :] = (top if i < 2 else low)[rows : rows + 128, cols : cols + 128]
    each(1, GROUP, lambda j: scatter(j).start())
    each(1, GROUP, lambda j: scatter(j).wait_recv())
    total = packed[my_slice, :].astype(F32)
    for j in range(1, GROUP):
        total = total + slots[j].astype(F32)
    own[...] = total
    full[my_slice, :] = total
    each(1, GROUP, lambda j: gather(j).start())
    each(1, GROUP, lambda j: gather(j).wait_recv())

    R, Q, M, Y = (rh, rl), (qh, ql), (mh, ml), (yh, yl)

    def eye(x):
        rows = lax.broadcasted_iota(jnp.int32, x.shape, 0)
        cols = lax.broadcasted_iota(jnp.int32, x.shape, 1)
        return rows == cols

    def poly():
        m = COEF_C * product(R, R) + COEF_B * (rh[...].astype(F32) + rl[...].astype(F32))
        put(M, m + jnp.where(eye(m), COEF_A, 0.0))

    def advance():
        put(Y, product(M, R))
        put(R, product(Y, M))

    trace = jnp.zeros((), F32)
    for n, (i, j) in enumerate(PIECES):
        if i == j:
            part = full[128 * n : 128 * n + 128, :]
            trace = trace + jnp.sum(jnp.where(eye(part), part, 0.0))
    scale2 = trace + EPSILON
    inverse = 1.0 / jnp.full((1, 128), scale2, F32)
    for n, (i, j) in enumerate(PIECES):
        part = full[128 * n : 128 * n + 128, :] * inverse
        high, low = split(part)
        rows, cols = slice(128 * i, 128 * i + 128), slice(128 * j, 128 * j + 128)
        rh[rows, cols] = high
        rl[rows, cols] = low
        if i != j:
            high, low = split(part.T)
            rh[cols, rows] = high
            rl[cols, rows] = low
    def first_factor():
        qh[...] = mh[...]
        ql[...] = ml[...]

    def sweep(i):
        poly()
        pl.when(i == 0)(first_factor)
        pl.when(i > 0)(lambda: put(Q, product(Q, M)))
        advance()

    each(0, ITERS - 1, sweep)
    poly()
    factor[...] = (product(Q, M) * (1.0 / jnp.sqrt(jnp.full((1, ROWS), scale2, F32)))).astype(BF16)

    def strip(c):
        chip = lax.rem(z // 2 + c, ZS // 2)
        rows = pl.ds(pl.multiple_of(chip * 128, 128), 128)
        upd[rows, :] = (0.2 * math.sqrt(COLS) * dot(factor[rows, :], held[...])).astype(BF16)

        def send(i):
            dest = chip * 8 + i // 2
            b = lax.rem(i, 2)
            pl.when(jnp.logical_or(dest != me, b != core))(lambda: backward(b, dest).start())

        each(0, 16, send)

    each(0, ZS // 2, strip)
    keep_backward.start()
    keep_moment.wait()
    each(1, GROUP, lambda j: scatter(j).wait_send())
    each(1, GROUP, lambda j: gather(j).wait_send())
    others(lambda other, i: forward_in(other, i).wait_send())
    keep_backward.wait()
    others(lambda other, i: backward_in(other, i).wait_send())
    others(lambda other, i: backward_in(other, i).wait_recv())


def exchange(gradient, momentum):
    matrix = pltpu.VMEM((ROWS, ROWS), BF16)
    staged = pltpu.VMEM(gradient.shape, BF16)
    dma = pltpu.SemaphoreType.DMA
    return pl.pallas_call(
        kernel,
        out_shape=(
            jax.ShapeDtypeStruct((OUT, BLOCK, WIDTH), BF16),
            jax.ShapeDtypeStruct(momentum.shape, BF16),
        ),
        in_specs=[pl.BlockSpec(memory_space=pltpu.HBM)] * 2,
        out_specs=[pl.BlockSpec(memory_space=pl.ANY)] * 2,
        scratch_shapes=[
            pltpu.VMEM((OUT, BLOCK, WIDTH), BF16),
            pltpu.VMEM((ROWS, WIDTH), BF16),
            pltpu.VMEM((ROWS, WIDTH), BF16),
            pltpu.VMEM((TALL, 128), BF16),
            pltpu.VMEM((GROUP, SLICE, 128), BF16),
            pltpu.VMEM((SLICE, 128), F32),
            pltpu.VMEM((TALL, 128), F32),
            *[matrix] * 9,
            staged, staged, staged,
            dma((2, OUT)), dma((2, OUT)), dma((2, OUT)), dma((2, OUT)),
            dma((GROUP,)), dma((GROUP,)), dma((GROUP,)), dma((GROUP,)),
            dma((2,)), dma((2,)), dma,
        ],
        compiler_params=pltpu.CompilerParams(
            collective_id=0, has_side_effects=True, vmem_limit_bytes=VMEM_LIMIT
        ),
        name="muon",
    )(gradient, momentum)


def on_device(weight, gradient, momentum):
    returned, momentum_next = exchange(gradient, momentum)
    weight_next = 0.9 * weight - 0.5 * returned[:, :, : weight.shape[2]].astype(F32)
    return (weight_next, momentum_next)


def solution(mesh):
    spec = P(None, "out", "inp")
    return jax.shard_map(
        on_device, mesh=mesh, in_specs=(spec, spec, spec), out_specs=(spec, spec), check_vma=False
    )
```

profile of v0, /device:TPU:1, one launch (start us, length us, event | category | flops | bytes accessed | tf_op | source)
XLA Modules:
  0.0 117.1 jit_solution(17111770294287218000)
XLA Ops:
  0.6 0.0 copy-start
  0.6 112.8 %muon.1 = (bf16[32,16,1792]{2,1,0:T(8,128)(2,1)S(1)}, bf16[32,16,1728]{2,1,0:T(8,128)(2,1)S(1)}) custom-call(bf16[32,16,1728]{2,1,0:T(8,128)(2,1)} %grad.1, bf16[32,16,1728]{2,1,0:T(8,128)(2,1)} %mom.1), custom_call_target="tpu_custom_call" | custom-call | tf_op jit(solution)/shard_map/muon/pallas_call | solution.py:310
  113.4 0.0 copy-done
  113.4 2.4 %multiply_subtract_fusion = f32[32,16,1728]{2,1,0:T(8,128)} fusion(f32[32,16,1728]{2,1,0:T(8,128)S(1)} %copy-done, bf16[32,16,1792]{2,1,0:T(8,128)(2,1)S(1)} %get-tuple-element.4), kind=kLoop, calls=%fused_computation | loop fusion | flops 3538944 | bytes 8847360 | tf_op jit(solution)/shard_map/sub | solution.py:341
  115.8 1.2 %copy.6 = bf16[32,16,1728]{2,1,0:T(8,128)(2,1)} copy(bf16[32,16,1728]{2,1,0:T(8,128)(2,1)S(1)} %get-tuple-element.9) | data formatting | bytes 3538944
Async XLA Ops:
  0.6 112.8 %copy-start = (f32[32,16,1728]{2,1,0:T(8,128)S(1)}, f32[32,16,1728]{2,1,0:T(8,128)}, u32[]{:S(2)}) copy-start(f32[32,16,1728]{2,1,0:T(8,128)} %param.3) | copy-start | bytes 10616836
where the time goes:
time: 119 us; the launch traced here: 117 us
  Pallas kernels  113 us (95%)
  other arithmetic  2.38 us (2%)
  local copies, waits for them, and re-layouts  1.23 us (1%)
    pallas_call x1, Pallas kernels, exchange(): pl.pallas_call(kernel, out_shape=(jax.ShapeDtypeStruct((OUT, BLOCK, WIDTH...  113 us
    sub x1, other arithmetic, on_device(): 0.9 * weight - 0.5 * returned[:, :, :weight.shape[2]].astype(F32)  2.38 us

commit v1 on v0

v1 whole, which is shorter than its diff:
```python
import functools
import math

import jax
import jax.numpy as jnp
from jax import lax
from jax.experimental import pallas as pl
from jax.experimental.pallas import tpu as pltpu
from jax.sharding import PartitionSpec as P

ITERS = 5
COLS = 13824
BETA = 0.95
EPSILON = 1e-06
COEF_A = 3.4445
COEF_B = -4.775
COEF_C = 2.0315

MESH = pl.DeviceIdType.MESH
BF16 = jnp.bfloat16
F32 = jnp.float32

ZS, YS, INP = 8, 4, 8
OUT = ZS * YS
XS = INP // 2
LOCAL = 2
BATCHES = 2 * LOCAL
ROWS = 512
BLOCK = 16
WIDTH = 1792
WIDE, SLIM = 512, 384
PIECES_OF = [(0, WIDE), (512, WIDE), (1024, SLIM), (1408, SLIM)]
GROUP = XS * YS
PIECES = [(i, j) for i in range(4) for j in range(i, 4)]
TALL = 128 * len(PIECES)
SLICE = TALL // GROUP
VMEM_LIMIT = 50 * 2**20


def dot(a, b):
    return lax.dot_general(a, b, (((1,), (0,)), ((), ())), preferred_element_type=F32)


def dot_t(a, b):
    return lax.dot_general(a, b, (((1,), (1,)), ((), ())), preferred_element_type=F32)


def split(x):
    high = x.astype(BF16)
    return high, (x - high.astype(F32)).astype(BF16)


def product(a, b):
    return dot(a[0][...], b[0][...]) + dot(a[0][...], b[1][...]) + dot(a[1][...], b[0][...])


def put(pair, x):
    high, low = split(x)
    pair[0][...] = high
    pair[1][...] = low


def kernel(
    grad, mom, ret, mom_next, src, held, upd, packed, slots, own, full, factor,
    rh, rl, qh, ql, mh, ml, yh, yl, grad_in, mom_in, mom_out,
    f_send, f_recv, b_send, b_recv, r_send, r_recv, g_send, g_recv, local, load, store,
):
    me = lax.axis_index("out")
    inp = lax.axis_index("inp")
    z, y = me // YS, lax.rem(me, YS)
    x, core = inp // 2, lax.rem(inp, 2)
    rank = y * XS + x
    width = grad.shape[2]

    def mine(l):
        return z * BATCHES + 2 * l + core

    loads = [
        pltpu.make_async_copy(grad, grad_in, load.at[0]),
        pltpu.make_async_copy(mom, mom_in, load.at[1]),
    ]
    for copy in loads:
        copy.start()

    def each(low, high, do):
        def body(i, c):
            do(i)
            return c

        lax.fori_loop(low, high, body, 0)

    def by_width(do):
        pl.when(y < 2)(lambda: do(WIDE, pl.multiple_of(y * WIDE, 128)))
        pl.when(y >= 2)(lambda: do(SLIM, pl.multiple_of(2 * WIDE + (y - 2) * SLIM, 128)))

    def clear():
        for l in range(LOCAL):
            for c in range(2):
                held[l, :, c * WIDE + SLIM : c * WIDE + WIDE] = jnp.zeros((ROWS, WIDE - SLIM), BF16)

    pl.when(y >= 2)(clear)

    def mate(j):
        other = lax.rem(rank + j, GROUP)
        return (z * YS + other // XS, 2 * lax.rem(other, XS) + core), other

    barrier = pltpu.get_barrier_semaphore()

    def greet(i):
        dest = lax.rem(me + i, OUT)
        for other in range(2):
            pl.semaphore_signal(barrier, inc=1, device_id=(dest, 2 * x + other), device_id_type=MESH)

    def greet_mate(j):
        pl.semaphore_signal(barrier, inc=1, device_id=mate(j)[0], device_id_type=MESH)

    each(1, OUT, greet)
    each(1, GROUP, greet_mate)
    pl.semaphore_signal(barrier, inc=1, device_id=(me, 2 * x + 1 - core), device_id_type=MESH)
    for copy in loads:
        copy.wait()

    def elementwise(k):
        g = grad_in[k].astype(F32)
        moment = BETA * mom_in[k].astype(F32) + g
        mom_out[k] = moment.astype(BF16)
        src[k, :, 0:width] = (g + BETA * moment).astype(BF16)
        src[k, :, width:WIDTH] = jnp.zeros((BLOCK, WIDTH - width), BF16)

    each(0, OUT, elementwise)
    keep_moment = pltpu.make_async_copy(mom_out, mom_next, store)
    keep_moment.start()
    pl.semaphore_wait(barrier, 2 * (OUT - 1) + GROUP - 1 + 1)

    def block(dest):
        return pl.ds(pl.multiple_of(dest * BLOCK, BLOCK), BLOCK)

    def part(which, wide):
        return pl.ds(pl.multiple_of(which * WIDE, 128), wide)

    def place(dest):
        return lax.rem(dest // YS - z + ZS, ZS) * YS + lax.rem(lax.rem(dest, YS) - y + YS, YS)

    def forward(b, chip, yd):
        dest = chip * YS + yd
        offset, wide = PIECES_OF[yd]
        return pltpu.make_async_remote_copy(
            src_ref=src.at[chip * BATCHES + b, :, offset : offset + wide],
            dst_ref=held.at[b // 2, block(me), part(core, wide)],
            send_sem=f_send.at[b, place(dest)],
            recv_sem=f_recv.at[b // 2 * 2 + core, place(dest)],
            device_id=(dest, 2 * x + b % 2),
            device_id_type=MESH,
        )

    def forward_in(l, other, i, wide):
        return pltpu.make_async_remote_copy(
            src_ref=src.at[0, :, 0:wide],
            dst_ref=held.at[l, block(0), part(0, wide)],
            send_sem=f_send.at[2 * l + other, i],
            recv_sem=f_recv.at[2 * l + other, i],
            device_id=(me, 2 * x + 1 - core),
            device_id_type=MESH,
        )

    def backward(l, b, dest, wide, offset):
        return pltpu.make_async_remote_copy(
            src_ref=upd.at[l, block(dest), part(b, wide)],
            dst_ref=ret.at[mine(l), :, pl.ds(offset, wide)],
            send_sem=b_send.at[2 * l + b, place(dest)],
            recv_sem=b_recv.at[2 * l + core, place(dest)],
            device_id=(dest, 2 * x + b),
            device_id_type=MESH,
        )

    def backward_in(l, other, i, wide):
        return pltpu.make_async_remote_copy(
            src_ref=upd.at[l, block(0), part(0, wide)],
            dst_ref=ret.at[0, :, 0:wide],
            send_sem=b_send.at[2 * l + other, i],
            recv_sem=b_recv.at[2 * l + other, i],
            device_id=(me, 2 * x + 1 - core),
            device_id_type=MESH,
        )

    def keep_forward(l, wide, offset):
        return pltpu.make_async_copy(
            src.at[mine(l), :, pl.ds(offset, wide)], held.at[l, block(me), part(core, wide)], local.at[0, l]
        )

    def keep_backward(l, wide, offset):
        return pltpu.make_async_copy(
            upd.at[l, block(me), part(core, wide)], ret.at[mine(l), :, pl.ds(offset, wide)], local.at[1, l]
        )

    my_slice = pl.ds(pl.multiple_of(rank * SLICE, 16), SLICE)

    def scatter(l, j):
        device, other = mate(j)
        return pltpu.make_async_remote_copy(
            src_ref=packed.at[l, pl.ds(pl.multiple_of(other * SLICE, 16), SLICE)],
            dst_ref=slots.at[l, j],
            send_sem=r_send.at[l, j],
            recv_sem=r_recv.at[l, j],
            device_id=device,
            device_id_type=MESH,
        )

    def gather(l, j):
        device, _ = mate(j)
        return pltpu.make_async_remote_copy(
            src_ref=own.at[l],
            dst_ref=full.at[l, my_slice],
            send_sem=g_send.at[l, j],
            recv_sem=g_recv.at[l, j],
            device_id=device,
            device_id_type=MESH,
        )

    def all_forward(b, do):
        def body(i):
            t = lax.rem(i, ZS)
            step = jnp.where(lax.rem(t, 2) == 1, (t + 1) // 2, ZS - t // 2)
            chip = lax.rem(z + step, ZS)
            for yd in range(YS):
                away = jnp.logical_or(chip * YS + yd != me, core != b % 2)
                pl.when(away)(lambda: do(forward(b, chip, yd)))

        each(1, ZS + 1, body)

    def others(do):
        for other in range(2):
            each(1, OUT, lambda i: do(other, i))
            pl.when(core != other)(lambda: do(other, 0))

    for b in range(BATCHES):
        all_forward(b, lambda copy: copy.start())
    for l in range(LOCAL):
        by_width(lambda wide, offset: keep_forward(l, wide, offset).start())

    def gram(l):
        by_width(lambda wide, offset: keep_forward(l, wide, offset).wait())
        by_width(lambda wide, offset: others(lambda other, i: forward_in(l, other, i, wide).wait_recv()))
        top = dot_t(held[l, 0:256, :], held[l]).astype(BF16)
        low = dot_t(held[l, 256:512, :], held[l, 256:512, :]).astype(BF16)
        for n, (i, j) in enumerate(PIECES):
            rows, cols = (128 * i, 128 * j) if i < 2 else (128 * i - 256, 128 * j - 256)
            packed[l, 128 * n : 128 * n + 128, :] = (top if i < 2 else low)[rows : rows + 128, cols : cols + 128]
        each(1, GROUP, lambda j: scatter(l, j).start())

    def reduce(l):
        each(1, GROUP, lambda j: scatter(l, j).wait_recv())
        total = packed[l, my_slice, :].astype(F32)
        for j in range(1, GROUP):
            total = total + slots[l, j].astype(F32)
        own[l] = total
        full[l, my_slice, :] = total
        each(1, GROUP, lambda j: gather(l, j).start())

    R, Q, M, Y = (rh, rl), (qh, ql), (mh, ml), (yh, yl)

    def eye(x):
        rows = lax.broadcasted_iota(jnp.int32, x.shape, 0)
        cols = lax.broadcasted_iota(jnp.int32, x.shape, 1)
        return rows == cols

    def poly():
        m = COEF_C * product(R, R) + COEF_B * (rh[...].astype(F32) + rl[...].astype(F32))
        put(M, m + jnp.where(eye(m), COEF_A, 0.0))

    def advance():
        put(Y, product(M, R))
        put(R, product(Y, M))

    def first_factor():
        qh[...] = mh[...]
        ql[...] = ml[...]

    def turn(l):
        each(1, GROUP, lambda j: gather(l, j).wait_recv())
        trace = jnp.zeros((), F32)
        for n, (i, j) in enumerate(PIECES):
            if i == j:
                piece = full[l, 128 * n : 128 * n + 128, :]
                trace = trace + jnp.sum(jnp.where(eye(piece), piece, 0.0))
        scale2 = trace + EPSILON
        inverse = 1.0 / jnp.full((1, 128), scale2, F32)
        for n, (i, j) in enumerate(PIECES):
            piece = full[l, 128 * n : 128 * n + 128, :] * inverse
            high, low = split(piece)
            rows, cols = slice(128 * i, 128 * i + 128), slice(128 * j, 128 * j + 128)
            rh[rows, cols] = high
            rl[rows, cols] = low
            if i != j:
                high, low = split(piece.T)
                rh[cols, rows] = high
                rl[cols, rows] = low

        def sweep(i):
            poly()
            pl.when(i == 0)(first_factor)
            pl.when(i > 0)(lambda: put(Q, product(Q, M)))
            advance()
            pl.when(jnp.logical_and(l == 0, i == 2))(lambda: gram(1))

        each(0, ITERS - 1, sweep)
        poly()
        factor[...] = (product(Q, M) * (1.0 / jnp.sqrt(jnp.full((1, ROWS), scale2, F32)))).astype(BF16)
        pl.when(l == 0)(lambda: reduce(1))

        def strip(c):
            chips = lax.rem(z // 2 + c, ZS // 2)
            rows = pl.ds(pl.multiple_of(chips * 128, 128), 128)
            upd[l, rows, :] = (0.2 * math.sqrt(COLS) * dot(factor[rows, :], held[l])).astype(BF16)

            def send(wide, offset):
                def one(i):
                    dest = chips * 8 + i // 2
                    b = lax.rem(i, 2)
                    away = jnp.logical_or(dest != me, b != core)
                    pl.when(away)(lambda: backward(l, b, dest, wide, offset).start())

                each(0, 16, one)

            by_width(send)

        each(0, ZS // 2, strip)
        by_width(lambda wide, offset: keep_backward(l, wide, offset).start())

    gram(0)
    reduce(0)
    each(0, LOCAL, turn)
    keep_moment.wait()
    for b in range(BATCHES):
        all_forward(b, lambda copy: copy.wait_send())
    for l in range(LOCAL):
        each(1, GROUP, lambda j: scatter(l, j).wait_send())
        each(1, GROUP, lambda j: gather(l, j).wait_send())
        by_width(lambda wide, offset: keep_backward(l, wide, offset).wait())
        by_width(lambda wide, offset: others(lambda other, i: backward_in(l, other, i, wide).wait_send()))
    for l in range(LOCAL):
        for other in range(2):
            for ys in range(YS):
                wide = PIECES_OF[ys][1]
                behind = lax.rem(y - ys + YS, YS)

                def arrive(step):
                    away = jnp.logical_or(step * YS + behind != 0, core != other)
                    pl.when(away)(lambda: backward_in(l, other, step * YS + behind, wide).wait_recv())

                each(0, ZS, arrive)


def exchange(gradient, momentum):
    matrix = pltpu.VMEM((ROWS, ROWS), BF16)
    staged = pltpu.VMEM(gradient.shape, BF16)
    dma = pltpu.SemaphoreType.DMA
    return pl.pallas_call(
        kernel,
        out_shape=(
            jax.ShapeDtypeStruct((OUT, BLOCK, WIDTH), BF16),
            jax.ShapeDtypeStruct(momentum.shape, BF16),
        ),
        in_specs=[pl.BlockSpec(memory_space=pltpu.HBM)] * 2,
        out_specs=[pl.BlockSpec(memory_space=pl.ANY)] * 2,
        scratch_shapes=[
            pltpu.VMEM((OUT, BLOCK, WIDTH), BF16),
            pltpu.VMEM((LOCAL, ROWS, 2 * WIDE), BF16),
            pltpu.VMEM((LOCAL, ROWS, 2 * WIDE), BF16),
            pltpu.VMEM((LOCAL, TALL, 128), BF16),
            pltpu.VMEM((LOCAL, GROUP, SLICE, 128), BF16),
            pltpu.VMEM((LOCAL, SLICE, 128), F32),
            pltpu.VMEM((LOCAL, TALL, 128), F32),
            *[matrix] * 9,
            staged, staged, staged,
            dma((BATCHES, OUT)), dma((BATCHES, OUT)), dma((BATCHES, OUT)), dma((BATCHES, OUT)),
            dma((LOCAL, GROUP)), dma((LOCAL, GROUP)), dma((LOCAL, GROUP)), dma((LOCAL, GROUP)),
            dma((2, LOCAL)), dma((2,)), dma,
        ],
        compiler_params=pltpu.CompilerParams(
            collective_id=0, has_side_effects=True, vmem_limit_bytes=VMEM_LIMIT
        ),
        name="muon",
    )(gradient, momentum)


def on_device(weight, gradient, momentum):
    returned, momentum_next = exchange(gradient, momentum)
    weight_next = 0.9 * weight - 0.5 * returned[:, :, : weight.shape[2]].astype(F32)
    return (weight_next, momentum_next)


def solution(mesh):
    spec = P(None, "out", "inp")
    return jax.shard_map(
        on_device, mesh=mesh, in_specs=(spec, spec, spec), out_specs=(spec, spec), check_vma=False
    )
```

time: 119 us -> 135 us (1.13)
  Pallas kernels: 113 us -> 129 us
    pallas_call x1, Pallas kernels: 113 us -> 129 us  [exchange(): pl.pallas_call(kernel, out_shape=(jax.ShapeDtypeStruct((OUT, BLOCK, WIDTH...]
where the time goes in v1:
time: 135 us; the launch traced here: 133 us
  Pallas kernels  129 us (96%)
  other arithmetic  2.38 us (2%)
    pallas_call x1, Pallas kernels, exchange(): pl.pallas_call(kernel, out_shape=(jax.ShapeDtypeStruct((OUT, BLOCK, WIDTH...  129 us

profile of v1, /device:TPU:1, one launch (start us, length us, event | category | flops | bytes accessed | tf_op | source)
XLA Modules:
  0.0 133.3 jit_solution(17357982356624852100)
XLA Ops:
  0.6 0.0 copy-start
  0.6 129.1 %muon.1 = (bf16[32,16,1792]{2,1,0:T(8,128)(2,1)S(1)}, bf16[32,16,1728]{2,1,0:T(8,128)(2,1)S(1)}) custom-call(bf16[32,16,1728]{2,1,0:T(8,128)(2,1)} %grad.1, bf16[32,16,1728]{2,1,0:T(8,128)(2,1)} %mom.1), custom_call_target="tpu_custom_call" | custom-call | tf_op jit(solution)/shard_map/muon/pallas_call | solution.py:358
  129.7 0.0 copy-done
  129.7 2.4 %multiply_subtract_fusion = f32[32,16,1728]{2,1,0:T(8,128)} fusion(f32[32,16,1728]{2,1,0:T(8,128)S(1)} %copy-done, bf16[32,16,1792]{2,1,0:T(8,128)(2,1)S(1)} %get-tuple-element.4), kind=kLoop, calls=%fused_computation | loop fusion | flops 3538944 | bytes 8847360 | tf_op jit(solution)/shard_map/sub | solution.py:389
  132.1 1.2 copy.6
Async XLA Ops:
  0.6 129.1 %copy-start = (f32[32,16,1728]{2,1,0:T(8,128)S(1)}, f32[32,16,1728]{2,1,0:T(8,128)}, u32[]{:S(2)}) copy-start(f32[32,16,1728]{2,1,0:T(8,128)} %param.3) | copy-start | bytes 10616836

commit v2 on v0

--- a/solution.py
+++ b/solution.py
@@ -207,9 +207,14 @@
             device_id_type=MESH,
         )
 
-    for b in range(2):
-        each(YS, YS + OUT - 1, lambda i: forward(b, partner(i)).start())
-        pl.when(core != b)(lambda: forward(b, me).start())
+    def send_on(low, high):
+        each(low, high, lambda i: forward(1, partner(i)).start())
+
+    each(YS, YS + OUT - 1, lambda i: forward(0, partner(i)).start())
+    pl.when(core != 0)(lambda: forward(0, me).start())
+    send_on(YS, 4 * YS)
+    pl.when(core != 1)(lambda: forward(1, me).start())
+    pl.when(core != 0)(lambda: send_on(4 * YS, YS + OUT - 1))
     keep_forward.start()
 
     def others(do):
@@ -225,6 +230,7 @@
         rows, cols = (128 * i, 128 * j) if i < 2 else (128 * i - 256, 128 * j - 256)
         packed[128 * n : 128 * n + 128, :] = (top if i < 2 else low)[rows : rows + 128, cols : cols + 128]
     each(1, GROUP, lambda j: scatter(j).start())
+    pl.when(core == 0)(lambda: send_on(4 * YS, 6 * YS))
     each(1, GROUP, lambda j: scatter(j).wait_recv())
     total = packed[my_slice, :].astype(F32)
     for j in range(1, GROUP):
@@ -232,6 +238,7 @@
     own[...] = total
     full[my_slice, :] = total
     each(1, GROUP, lambda j: gather(j).start())
+    pl.when(core == 0)(lambda: send_on(6 * YS, YS + OUT - 1))
     each(1, GROUP, lambda j: gather(j).wait_recv())
 
     R, Q, M, Y = (rh, rl), (qh, ql), (mh, ml), (yh, yl)

time: 119 us -> 120 us (level); the launches traced: 117 us -> 120 us
  Pallas kernels: 113 us -> 115 us
    pallas_call x1, Pallas kernels: 113 us -> 115 us  [exchange(): pl.pallas_call(kernel, out_shape=(jax.ShapeDtypeStruct((OUT, BLOCK, WIDTH...]
where the time goes in v2:
time: 120 us
  Pallas kernels  115 us (96%)
  other arithmetic  2.38 us (2%)
  local copies, waits for them, and re-layouts  1.23 us (1%)
    pallas_call x1, Pallas kernels, exchange(): pl.pallas_call(kernel, out_shape=(jax.ShapeDtypeStruct((OUT, BLOCK, WIDTH...  115 us

profile of v2, /device:TPU:1, one launch (start us, length us, event | category | flops | bytes accessed | tf_op | source)
XLA Modules:
  0.0 119.5 jit_solution(4196996966153211838)
XLA Ops:
  0.6 0.0 copy-start
  0.6 115.3 %muon.1 = (bf16[32,16,1792]{2,1,0:T(8,128)(2,1)S(1)}, bf16[32,16,1728]{2,1,0:T(8,128)(2,1)S(1)}) custom-call(bf16[32,16,1728]{2,1,0:T(8,128)(2,1)} %grad.1, bf16[32,16,1728]{2,1,0:T(8,128)(2,1)} %mom.1), custom_call_target="tpu_custom_call" | custom-call | tf_op jit(solution)/shard_map/muon/pallas_call | solution.py:317
  115.9 0.0 copy-done
  115.9 2.4 %multiply_subtract_fusion = f32[32,16,1728]{2,1,0:T(8,128)} fusion(f32[32,16,1728]{2,1,0:T(8,128)S(1)} %copy-done, bf16[32,16,1792]{2,1,0:T(8,128)(2,1)S(1)} %get-tuple-element.4), kind=kLoop, calls=%fused_computation | loop fusion | flops 3538944 | bytes 8847360 | tf_op jit(solution)/shard_map/sub | solution.py:348
  118.3 1.2 %copy.6 = bf16[32,16,1728]{2,1,0:T(8,128)(2,1)} copy(bf16[32,16,1728]{2,1,0:T(8,128)(2,1)S(1)} %get-tuple-element.9) | data formatting | bytes 3538944
Async XLA Ops:
  0.6 115.3 %copy-start = (f32[32,16,1728]{2,1,0:T(8,128)S(1)}, f32[32,16,1728]{2,1,0:T(8,128)}, u32[]{:S(2)}) copy-start(f32[32,16,1728]{2,1,0:T(8,128)} %param.3) | copy-start | bytes 10616836

commit v3 on v0

--- a/solution.py
+++ b/solution.py
@@ -27,7 +27,8 @@
 BLOCK = 16
 WIDTH = 1792
 HALF = WIDTH // BATCHES
-GROUP = INP // 2 * BATCHES
+XS = INP // 2
+GROUP = XS * BATCHES
 PIECES = [(i, j) for i in range(4) for j in range(i, 4)]
 TALL = 128 * len(PIECES)
 SLICE = TALL // GROUP
@@ -85,8 +86,9 @@
         return lax.rem(z + step, ZS) * YS + lax.rem(y + lax.rem(at, YS), YS)
 
     def mate(j):
-        other = lax.rem(rank + j, GROUP)
-        return (team * BATCHES + other // (INP // 2), 2 * lax.rem(other, INP // 2) + core), other
+        other_seat = lax.rem(seat + j // XS, BATCHES)
+        other_x = lax.rem(x + lax.rem(j, XS), XS)
+        return (team * BATCHES + other_seat, 2 * other_x + core), other_seat * XS + other_x
 
     barrier = pltpu.get_barrier_semaphore()
 
@@ -224,14 +226,16 @@
     for n, (i, j) in enumerate(PIECES):
         rows, cols = (128 * i, 128 * j) if i < 2 else (128 * i - 256, 128 * j - 256)
         packed[128 * n : 128 * n + 128, :] = (top if i < 2 else low)[rows : rows + 128, cols : cols + 128]
-    each(1, GROUP, lambda j: scatter(j).start())
+    each(XS, GROUP, lambda j: scatter(j).start())
+    each(1, XS, lambda j: scatter(j).start())
     each(1, GROUP, lambda j: scatter(j).wait_recv())
     total = packed[my_slice, :].astype(F32)
     for j in range(1, GROUP):
         total = total + slots[j].astype(F32)
     own[...] = total
     full[my_slice, :] = total
-    each(1, GROUP, lambda j: gather(j).start())
+    each(XS, GROUP, lambda j: gather(j).start())
+    each(1, XS, lambda j: gather(j).start())
     each(1, GROUP, lambda j: gather(j).wait_recv())
 
     R, Q, M, Y = (rh, rl), (qh, ql), (mh, ml), (yh, yl)

time: 119 us -> 119 us (level)
  no operation moved by 1% of the time
where the time goes in v3:
time: 119 us; the launch traced here: 117 us
  Pallas kernels  113 us (95%)
  other arithmetic  2.38 us (2%)
  local copies, waits for them, and re-layouts  1.23 us (1%)
    pallas_call x1, Pallas kernels, exchange(): pl.pallas_call(kernel, out_shape=(jax.ShapeDtypeStruct((OUT, BLOCK, WIDTH...  113 us
    sub x1, other arithmetic, on_device(): 0.9 * weight - 0.5 * returned[:, :, :weight.shape[2]].astype(F32)  2.38 us

profile of v3, /device:TPU:1, one launch (start us, length us, event | category | flops | bytes accessed | tf_op | source)
XLA Modules:
  0.0 117.1 jit_solution(7762732467206988042)
XLA Ops:
  0.6 0.0 copy-start
  0.6 112.8 %muon.1 = (bf16[32,16,1792]{2,1,0:T(8,128)(2,1)S(1)}, bf16[32,16,1728]{2,1,0:T(8,128)(2,1)S(1)}) custom-call(bf16[32,16,1728]{2,1,0:T(8,128)(2,1)} %grad.1, bf16[32,16,1728]{2,1,0:T(8,128)(2,1)} %mom.1), custom_call_target="tpu_custom_call" | custom-call | tf_op jit(solution)/shard_map/muon/pallas_call | solution.py:314
  113.5 0.0 copy-done
  113.5 2.4 %multiply_subtract_fusion = f32[32,16,1728]{2,1,0:T(8,128)} fusion(f32[32,16,1728]{2,1,0:T(8,128)S(1)} %copy-done, bf16[32,16,1792]{2,1,0:T(8,128)(2,1)S(1)} %get-tuple-element.4), kind=kLoop, calls=%fused_computation | loop fusion | flops 3538944 | bytes 8847360 | tf_op jit(solution)/shard_map/sub | solution.py:345
  115.9 1.2 %copy.6 = bf16[32,16,1728]{2,1,0:T(8,128)(2,1)} copy(bf16[32,16,1728]{2,1,0:T(8,128)(2,1)S(1)} %get-tuple-element.9) | data formatting | bytes 3538944
Async XLA Ops:
  0.6 112.8 %copy-start = (f32[32,16,1728]{2,1,0:T(8,128)S(1)}, f32[32,16,1728]{2,1,0:T(8,128)}, u32[]{:S(2)}) copy-start(f32[32,16,1728]{2,1,0:T(8,128)} %param.3) | copy-start | bytes 10616836
